TPU v7x, 256 devices: a whole 4x4x8 slice. The times are simulated.
256 devices in a mesh: samp: 8 (over x, core), state: 32 (over z, y).
Axes of the slice: x: 4, y: 4, z: 8, core: 2. Of those that a mesh axis runs over, the one named last changes fastest.
Arguments:
- components: bfloat16 [64, 262144], P(None, 'samp'), may hold values from -96 to 96
- coefficients: bfloat16 [64, 4096], P(None, 'state'), may hold values from -1.5 to 1.5
- block_window: int32 [2048], P('samp'), may hold values from 0 to 4095
- block_fill: int32 [2048], P('samp'), may hold values from 1 to 128
Outputs:
- free_energy: float32 [4096], P('state')
- log_denom: float32 [262144], P('samp')
Inputs may be any that keep to these rules, and one draw needn't show every extreme that they name: `block_window`: blocks of one generating state may stand anywhere; some states generate no block.
All inputs are finite; a program needn't handle non-finite values.
Results may differ from a plain program's by a relative error of at most 0.0003.
Values may be sent and summed in bfloat16 or wider, within the bound.
No kernel may reach another device: no remote copies, remote signals or barrier semaphores. Data moves between devices by JAX's collectives and lax.ppermute only.
A program may use at most 128 MiB of HBM per device.

v0:
```python
import functools

import jax
import jax.numpy as jnp
from jax import lax
from jax.experimental import pallas as pl
from jax.experimental.pallas import tpu as pltpu
from jax.sharding import Mesh
from jax.sharding import PartitionSpec as P


BLOCK = 128
LANES = 128
COMP = 64
TILE = 256
PARTS = 3
LOG2E = 1.4426950408889634
LN2 = 0.6931471805599453
CHUNK = 512
TAIL = 16
LEAST = 1e-25
SPREAD = 72.0
SMALL_ROWS = 8
SMALL = (SMALL_ROWS - 1) * LANES - 1
STATE = ("state_0", "state_1")
SAMP = ("samp_0", "samp_1")
NEGATIVE = -1e30
BF16 = jnp.bfloat16
F32 = jnp.float32


def exchanged(copies, axes):
    return lax.all_to_all(copies, axes, split_axis=0, concat_axis=0, tiled=True)


def copies_of_each(x, axes):
    return exchanged(jnp.broadcast_to(x, (lax.axis_size(axes), *x.shape)), axes)


def iota(shape, dim):
    return lax.broadcasted_iota(jnp.int32, shape, dim)


def dot_nt(a, b):
    return lax.dot_general(a, b, (((1,), (1,)), ((), ())), preferred_element_type=F32)


def dot(a, b):
    return jnp.dot(a, b, preferred_element_type=F32)


def three_parts(x):
    high = x.astype(BF16).astype(F32)
    rest = x - high
    middle = rest.astype(BF16).astype(F32)
    return high, middle, rest - middle


def log_sum(logs):
    highest = jnp.max(logs, axis=0)
    return highest + jnp.log(jnp.sum(jnp.exp(logs - highest[None]), axis=0))


def log_sum_pieces(logs_ref):
    pieces = logs_ref.shape[0]
    highest = functools.reduce(jnp.maximum, [logs_ref[p] for p in range(pieces)])
    totals = functools.reduce(jnp.add, [jnp.exp(logs_ref[p] - highest) for p in range(pieces)])
    return highest + jnp.log(totals)


def chunk(c):
    return pl.ds(c * CHUNK if isinstance(c, int) else pl.multiple_of(c * CHUNK, CHUNK), CHUNK)


def halves(combine, x):
    return x if x.shape[1] == LANES else combine(x[:, :LANES], x[:, LANES:])


def used_tile(coefs_ref, tails_ref, j):
    width = LANES if isinstance(j, int) and j == SMALL_ROWS * LANES // TILE - 1 else TILE
    return whole_tile(coefs_ref[j], tails_ref[j])[:, :width]


def points_kernel(spot_ref, own_ref, block_ref, head_ref, points_ref, dead_ref):
    rows = points_ref.shape[0]
    half = COMP // 2
    own = pl.multiple_of(spot_ref[1] * half, half)
    lane = iota((LANES, LANES - COMP), 1)
    ones = jnp.where((lane >= 3) & (lane < 6), 1.0, 0.0)
    for b in range(rows // LANES):
        at = slice(b * LANES, (b + 1) * LANES)
        mine = block_ref[pl.ds(own, half), at].astype(F32)
        other = block_ref[pl.ds(pl.multiple_of(half - own, half), half), at].astype(F32)
        high, middle, low = three_parts(jnp.concatenate([mine, other], 0).T * -LOG2E)
        head_ref[at, :] = jnp.concatenate([high, middle], 1).astype(BF16)
        points_ref[at, :] = jnp.concatenate([low, ones], 1).astype(BF16)
        fills = own_ref[0, 1:2, :]
        chosen = iota(fills.shape, 1) == spot_ref[0] * (rows // BLOCK) + b
        fill = jnp.sum(jnp.where(chosen, fills.astype(F32), 0.0), axis=1, keepdims=True)
        dead_ref[at, :] = jnp.where(iota((BLOCK, LANES), 0).astype(F32) < fill, 0.0, NEGATIVE)


def count_kernel(*refs):
    blocks_refs, (place_ref, meta_ref, digits_ref) = refs[:-3], refs[-3:]
    groups = place_ref.shape[0]
    width = blocks_refs[0].shape[2]
    counts = jnp.zeros((groups, LANES), F32)
    for blocks_ref, s in [(r, s) for r in blocks_refs for s in range(r.shape[0])]:
        window = blocks_ref[s, 0:1, :]
        fill = blocks_ref[s, 1:2, :]
        of_group = jnp.where(iota((groups, width), 0) == window >> 7, fill, 0).astype(F32).astype(BF16)
        of_lane = jnp.where(iota((LANES, width), 0) == (window & 127), 1.0, 0.0).astype(BF16)
        counts = counts + dot_nt(of_group, of_lane)
    counted = counts > 0
    packed = jnp.where(counted, 1.0, 0.0).astype(BF16)
    before = jnp.where(iota((LANES, LANES), 0) < iota((LANES, LANES), 1), 1.0, 0.0).astype(BF16)
    within = dot(packed, before)
    total = dot(packed, jnp.ones((LANES, LANES), BF16))
    earlier = jnp.where(iota((groups, groups), 1) < iota((groups, groups), 0), 1.0, 0.0).astype(BF16)
    offset_int = dot(earlier, total.astype(BF16)).astype(jnp.int32)
    within_int = within.astype(jnp.int32)
    place_ref[...] = jnp.where(counted, (offset_int & 127) + within_int, -1)
    meta_ref[0:groups, :] = offset_int >> 7
    everything = jnp.sum(total, axis=0, keepdims=True).astype(jnp.int32)
    meta_ref[groups : groups + 8, :] = jnp.broadcast_to(everything, (8, LANES))
    counts_int = counts.astype(jnp.int32)
    digits = [d.astype(F32) for d in (counts_int >> 14, (counts_int >> 7) & 127, counts_int & 127)]
    row = iota((TAIL, LANES), 0)
    for t in range(groups):
        rows = jnp.zeros((TAIL, LANES), F32)
        for k, digit in enumerate(digits):
            rows = jnp.where(row == k, digit[t : t + 1, :], rows)
        digits_ref[t] = rows.astype(BF16)


def tail_rows(weight):
    row = iota((TAIL, TILE), 0)
    rows = jnp.where(row < 3, 1.0, 0.0)
    if weight is not None:
        for k, part in enumerate(three_parts(weight)):
            rows = jnp.where(row == 3 + k, part, rows)
    return jnp.concatenate([rows.astype(BF16), jnp.zeros((LANES - COMP - TAIL, TILE), BF16)], 0)


def whole_tile(coefs, tail):
    return jnp.concatenate([coefs] * PARTS + [tail], 0)


def against(head_ref, points_ref, c, tile):
    return dot(jnp.concatenate([head_ref[chunk(c), :], points_ref[chunk(c), :]], 1), tile)


def with_shift(points, shift):
    lane = iota(points.shape, 1)
    for k, part in enumerate(three_parts(shift)):
        points = jnp.where(lane == COMP + k, part, points)
    return points


def tile_row(rows, j):
    return jnp.concatenate([rows[2 * j : 2 * j + 1, :], rows[2 * j + 1 : 2 * j + 2, :]], 1)


def over_tiles(tile_count, body, carry):
    if tile_count * TILE == SMALL_ROWS * LANES:
        for j in range(tile_count):
            carry = body(j, carry)
        return carry
    return lax.fori_loop(0, tile_count, body, carry)


def exact_denominators(c, head_ref, points_ref, coefs_ref, tails_ref, energy_ref):
    def find(j, top):
        exponents = against(head_ref, points_ref, c, used_tile(coefs_ref, tails_ref, j))
        energy_ref[j, :, : exponents.shape[1]] = exponents
        return jnp.maximum(top, halves(jnp.maximum, exponents))

    tile_count = coefs_ref.shape[0]
    top = over_tiles(tile_count, find, jnp.full((CHUNK, LANES), 4 * NEGATIVE, F32))
    top = jnp.max(top, axis=1, keepdims=True)

    def add(j, sums):
        width = used_tile(coefs_ref, tails_ref, j).shape[1]
        return sums + halves(jnp.add, jnp.exp2(energy_ref[j, :, :width] - top))

    sums = over_tiles(tile_count, add, jnp.zeros((CHUNK, LANES), F32))
    return jnp.broadcast_to(top + jnp.log2(jnp.sum(sums, axis=1, keepdims=True)), (CHUNK, LANES))


def near_denominators(c, base_ref, head_ref, anchored_ref, coefs_ref, tails_ref):
    def add(j, sums):
        tile = used_tile(coefs_ref, tails_ref, j)
        return sums + halves(jnp.add, jnp.exp2(against(head_ref, anchored_ref, c, tile)))

    sums = over_tiles(coefs_ref.shape[0], add, jnp.zeros((CHUNK, LANES), F32))
    return base_ref[chunk(c), :] + jnp.log2(jnp.sum(sums, axis=1, keepdims=True))


def put_live(c, points_ref, logden, live_ref, dead_ref):
    shift = dead_ref[chunk(c), :] - logden
    live_ref[chunk(c), :] = with_shift(points_ref[chunk(c), :].astype(F32), shift).astype(BF16)


def each_chunk(rows, body):
    def one(c, carry):
        body(c)
        return carry

    lax.fori_loop(0, rows // CHUNK, one, 0)


def exponents_and_highest(tile, head_ref, live_ref, exponent_ref):
    highest = None
    for c in range(live_ref.shape[0] // CHUNK):
        exponents = against(head_ref, live_ref, c, tile)
        exponent_ref[chunk(c), :] = exponents
        top = jnp.max(exponents.reshape(CHUNK // 8, 8, TILE), axis=0)
        highest = top if highest is None else jnp.maximum(highest, top)
    return jnp.max(highest, axis=0, keepdims=True)


def log_of_sum(highest, exponent_ref):
    totals = jnp.zeros((8, TILE), F32)
    for c in range(exponent_ref.shape[0] // CHUNK):
        grown = jnp.exp2(exponent_ref[chunk(c), :] - highest)
        totals = totals + jnp.sum(grown.reshape(CHUNK // 8, 8, TILE), axis=0)
    return highest + jnp.log2(jnp.sum(totals, axis=0, keepdims=True))


def put_rows(logs_ref, first, logs):
    logs = logs * LN2
    logs_ref[pl.ds(first, 1), :] = logs[:, :LANES]
    logs_ref[pl.ds(first + 1, 1), :] = logs[:, LANES:]


def counted_log_sums(weight_ref, coefs_ref, tails_ref, head_ref, live_ref, exponent_ref, logs_ref, low_ref):
    low_ref[...] = jnp.zeros(low_ref.shape, F32)
    logs_ref[0 : weight_ref.shape[0], :] = jnp.zeros(weight_ref.shape, F32)

    def finish(j, logs):
        weight = jnp.concatenate([weight_ref[pl.ds(2 * j, 1), :], weight_ref[pl.ds(2 * j + 1, 1), :]], 1)
        valid = weight > NEGATIVE / 2
        put_rows(logs_ref, 2 * j, jnp.where(valid, logs - weight, 0.0))
        return valid

    def one(i, carry):
        for k in range(2):
            j = 2 * i + k
            totals = jnp.zeros((8, TILE), F32)
            tile = whole_tile(coefs_ref[j], tails_ref[j])
            for c in range(live_ref.shape[0] // CHUNK):
                grown = jnp.exp2(against(head_ref, live_ref, c, tile))
                totals = totals + jnp.sum(grown.reshape(CHUNK // 8, 8, TILE), axis=0)
            totals = jnp.sum(totals, axis=0, keepdims=True)
            valid = finish(j, jnp.log2(totals))
            low_ref[0:1, :] = jnp.maximum(low_ref[0:1, :], jnp.where(valid & (totals < LEAST), 1.0, 0.0))
        return carry

    lax.fori_loop(0, coefs_ref.shape[0] // 2, one, 0)

    @pl.when(jnp.max(low_ref[...]) > 0)
    def _():
        def again(j, carry):
            highest = exponents_and_highest(whole_tile(coefs_ref[j], tails_ref[j]), head_ref, live_ref, exponent_ref)
            finish(j, log_of_sum(highest, exponent_ref))
            return carry

        lax.fori_loop(0, coefs_ref.shape[0], again, 0)


def weighted_tails(logs, log_count_ref, tails_ref, weight_ref):
    log_count = log_count_ref[...]
    valid = log_count > NEGATIVE / 2
    free = jnp.where(valid, logs * -LOG2E, 4 * NEGATIVE)
    highest = jnp.max(jnp.max(free, axis=0, keepdims=True), axis=1, keepdims=True)
    free = jnp.where(valid, free - highest, 0.0)
    weight = log_count + free
    weight_ref[...] = weight
    for j in range(tails_ref.shape[0]):
        tails_ref[j] = tail_rows(tile_row(weight, j))
    return highest, jnp.min(free)


def first_kernel(
    meta_ref, mine_ref, other_ref, place_ref, digits_ref, head_ref, points_ref, dead_ref,
    logs_ref, log_count_ref, coefs_ref, anchored_ref, base_ref,
    tails_ref, packed_ref, energy_ref, live_ref, exponent_ref, low_ref, rows_ref,
):
    groups = mine_ref.shape[0]
    packed_ref[...] = jnp.zeros(packed_ref.shape, F32)
    for t in range(groups):
        chosen = jnp.where(iota((2 * LANES, LANES), 0) == place_ref[t : t + 1, :], 1.0, 0.0).astype(BF16)
        moved = dot_nt(jnp.concatenate([mine_ref[t], other_ref[t], digits_ref[t]], 0), chosen)
        at = meta_ref[t]
        packed_ref[at] += moved[:, :LANES]
        packed_ref[at + 1] += moved[:, LANES:]
    for h in range(log_count_ref.shape[0]):
        digits = [packed_ref[h, COMP + k : COMP + k + 1, :] for k in range(3)]
        counts = digits[0] * 16384.0 + digits[1] * 128.0 + digits[2]
        log_count_ref[h : h + 1, :] = jnp.where(counts > 0, jnp.log2(jnp.maximum(counts, 1.0)), NEGATIVE)
    log_count = log_count_ref[...]
    for j in range(coefs_ref.shape[0]):
        coefs_ref[j] = jnp.concatenate([packed_ref[2 * j, 0:COMP, :], packed_ref[2 * j + 1, 0:COMP, :]], 1).astype(BF16)
        tails_ref[j] = tail_rows(tile_row(log_count, j))

    def denominators(c):
        logden = exact_denominators(c, head_ref, points_ref, coefs_ref, tails_ref, energy_ref)
        base_ref[chunk(c), :] = logden
        anchored_ref[chunk(c), :] = with_shift(points_ref[chunk(c), :].astype(F32), -logden).astype(BF16)
        put_live(c, points_ref, logden, live_ref, dead_ref)

    each_chunk(points_ref.shape[0], denominators)
    counted_log_sums(
        log_count_ref, coefs_ref, tails_ref, head_ref, live_ref, exponent_ref, rows_ref, low_ref
    )
    logs_ref[...] = jnp.broadcast_to(rows_ref[...][None], logs_ref.shape)


def new_denominators(least, base_ref, head_ref, anchored_ref, points_ref, coefs_ref, tails_ref, energy_ref, put):
    rows = points_ref.shape[0]
    near = least > -SPREAD

    @pl.when(near)
    def _():
        each_chunk(
            rows,
            lambda c: put(c, near_denominators(c, base_ref, head_ref, anchored_ref, coefs_ref, tails_ref)),
        )

    @pl.when(jnp.logical_not(near))
    def _():
        each_chunk(
            rows, lambda c: put(c, exact_denominators(c, head_ref, points_ref, coefs_ref, tails_ref, energy_ref))
        )


def places(slot_rows):
    if slot_rows == SMALL_ROWS:
        return (slot_rows - 1, slot_rows - 2), LANES - 1
    return (slot_rows, slot_rows + 1), 0


def put_message(logs, slot_rows, message_ref):
    (own_row, zero_row), zero_lane = places(slot_rows)
    rows = message_ref.shape[1]
    common = logs[0:slot_rows, :]
    if rows > slot_rows:
        common = jnp.concatenate([common, jnp.zeros((rows - slot_rows, LANES), F32)], 0)
    row, lane = iota(common.shape, 0), iota(common.shape, 1)
    common = jnp.where((row == zero_row) & (lane == zero_lane), logs[slot_rows : slot_rows + 1, 0:1], common)
    for t in range(message_ref.shape[0]):
        own = logs[slot_rows + t : slot_rows + t + 1, :]
        message_ref[t] = jnp.where(row == own_row, own, common)


def second_kernel(
    logs_in_ref, mine_ref, other_ref, log_count_ref, coefs_ref, head_ref, points_ref, dead_ref, anchored_ref,
    base_ref,
    message_ref,
    tails_ref, weight_ref, energy_ref, live_ref, exponent_ref, low_ref, rows_ref,
):
    groups = mine_ref.shape[0]
    slot_rows = weight_ref.shape[0]
    logs = log_sum_pieces(logs_in_ref)
    _, least = weighted_tails(logs, log_count_ref, tails_ref, weight_ref)
    new_denominators(
        least, base_ref, head_ref, anchored_ref, points_ref, coefs_ref, tails_ref, energy_ref,
        lambda c, logden: put_live(c, points_ref, logden, live_ref, dead_ref),
    )
    counted_log_sums(
        weight_ref, coefs_ref, tails_ref, head_ref, live_ref, exponent_ref, rows_ref, low_ref
    )
    tail = tail_rows(None)
    last = groups * LANES // TILE - 1

    def every_tile(t):
        parts = [jnp.concatenate([mine_ref[2 * t + k], other_ref[2 * t + k]], 0) for k in range(2)]
        return whole_tile(jnp.concatenate(parts, 1), tail)

    def step(t, highest):
        tile = every_tile(jnp.minimum(t + 1, last))
        totals = jnp.zeros((8, TILE), F32)
        tops = []
        for c in range(live_ref.shape[0] // CHUNK):
            grown = jnp.exp2(exponent_ref[chunk(c), :] - highest)
            totals = totals + jnp.sum(grown.reshape(CHUNK // 8, 8, TILE), axis=0)
            exponents = against(head_ref, live_ref, c, tile)
            exponent_ref[chunk(c), :] = exponents
            tops.append(jnp.max(exponents.reshape(CHUNK // 8, 8, TILE), axis=0))
        logs = highest + jnp.log2(jnp.sum(totals, axis=0, keepdims=True))
        put_rows(rows_ref, slot_rows + 2 * t, logs)
        return jnp.max(functools.reduce(jnp.maximum, tops), axis=0, keepdims=True)

    start = exponents_and_highest(every_tile(0), head_ref, live_ref, exponent_ref)
    lax.fori_loop(0, last + 1, step, start, unroll=4)
    put_message(rows_ref[...], slot_rows, message_ref)


def third_kernel(
    logs_in_ref, log_count_ref, coefs_ref, head_ref, points_ref, anchored_ref, base_ref,
    free_ref, logden_ref,
    tails_ref, weight_ref, energy_ref, totals_ref,
):
    slot_rows = weight_ref.shape[0]
    logs = log_sum_pieces(logs_in_ref)
    (own_row, zero_row), zero_lane = places(slot_rows)
    zero = logs[zero_row : zero_row + 1, zero_lane : zero_lane + 1]
    free_ref[...] = zero - logs[own_row : own_row + 1, :]
    highest, least = weighted_tails(logs[:slot_rows], log_count_ref, tails_ref, weight_ref)

    def put(c, logden):
        totals_ref[chunk(c), :] = logden

    new_denominators(
        least, base_ref, head_ref, anchored_ref, points_ref, coefs_ref, tails_ref, energy_ref, put
    )
    turned = [totals_ref[pl.ds(b * LANES, LANES), :].T[0:1, :] for b in range(points_ref.shape[0] // LANES)]
    logden = (jnp.concatenate(turned, 0) + highest) * LN2 + zero
    logden_ref[...] = jnp.broadcast_to(logden[None], logden_ref.shape)


def iterated(slot_rows, meta, mine, other, place, digits, head, points, dead):
    samps = lax.axis_size(SAMP)
    groups = mine.shape[0]
    rows = points.shape[0]
    tile_count = slot_rows * LANES // TILE
    shape = jax.ShapeDtypeStruct
    vmem = pl.BlockSpec(memory_space=pltpu.VMEM)
    smem = pl.BlockSpec(memory_space=pltpu.SMEM)
    params = pltpu.CompilerParams(vmem_limit_bytes=24 << 20)
    tails_work = pltpu.VMEM((tile_count, LANES - COMP, TILE), BF16)
    weight_work = pltpu.VMEM((slot_rows, LANES), F32)
    energy_work = pltpu.VMEM((tile_count, CHUNK, TILE), F32)
    live_work = pltpu.VMEM((rows, LANES), BF16)
    exponent_work = pltpu.VMEM((rows, TILE), F32)
    low_work = pltpu.VMEM((8, TILE), F32)
    logs, log_count, coefs, anchored, base = pl.pallas_call(
        first_kernel,
        out_shape=(
            shape((samps, slot_rows, LANES), F32), shape((slot_rows, LANES), F32), shape((tile_count, COMP, TILE), BF16), shape((rows, LANES), BF16),
            shape((rows, LANES), F32),
        ),
        in_specs=[smem] + [vmem] * 7, out_specs=(vmem,) * 5,
        scratch_shapes=[
            tails_work, pltpu.VMEM((slot_rows + 2, COMP + TAIL, LANES), F32), energy_work, live_work, exponent_work, low_work,
            weight_work,
        ],
        compiler_params=params, name="first",
    )(meta, mine, other, place, digits, head, points, dead)
    logs = log_sum(exchanged(logs, SAMP))
    logs = copies_of_each(logs, STATE)
    logs = pl.pallas_call(
        second_kernel,
        out_shape=shape((groups, slot_rows if slot_rows == SMALL_ROWS else slot_rows + 8, LANES), F32),
        in_specs=[vmem] * 10, out_specs=vmem,
        scratch_shapes=[
            tails_work, weight_work, energy_work, live_work, exponent_work,
            low_work, pltpu.VMEM((slot_rows + groups, LANES), F32),
        ],
        compiler_params=params, name="second",
    )(logs, mine, other, log_count, coefs, head, points, dead, anchored, base)
    logs = copies_of_each(log_sum(exchanged(logs, STATE)), SAMP)
    return pl.pallas_call(
        third_kernel,
        out_shape=(shape((1, LANES), F32), shape((groups, rows // LANES, LANES), F32)),
        in_specs=[vmem] * 7, out_specs=(vmem, vmem),
        scratch_shapes=[tails_work, weight_work, energy_work, pltpu.VMEM((rows, LANES), F32)],
        compiler_params=params, name="third",
    )(logs, log_count, coefs, head, points, anchored, base)


def shards(components, coefficients, block_window, block_fill):
    groups = lax.axis_size(STATE)
    samps = lax.axis_size(SAMP)
    position = lax.axis_index(STATE)
    core = lax.axis_index(SAMP[1])
    rows = components.shape[1] // groups
    slot_rows = min(samps * block_window.shape[0] // LANES, groups)
    shape = jax.ShapeDtypeStruct
    vmem = pl.BlockSpec(memory_space=pltpu.VMEM)
    params = pltpu.CompilerParams(vmem_limit_bytes=24 << 20)
    spot = jnp.stack([position, core]).astype(jnp.int32)

    half = COMP // 2
    mine = copies_of_each(lax.dynamic_slice_in_dim(coefficients, core * half, half, 0), STATE)
    pair = jnp.stack([block_window, block_fill])[None]
    blocks = jnp.concatenate([pair, lax.ppermute(pair, SAMP[1], [(0, 1), (1, 0)])], 0)
    along = lax.axis_size(SAMP[0])
    turns = [[(i, (i + k) % along) for i in range(along)] for k in range(1, along)]
    pieces = [blocks] + [lax.ppermute(blocks, SAMP[0], turn) for turn in turns]
    head, points, dead = pl.pallas_call(
        points_kernel,
        out_shape=(shape((rows, LANES), BF16), shape((rows, LANES), BF16), shape((rows, LANES), F32)),
        grid_spec=pltpu.PrefetchScalarGridSpec(
            num_scalar_prefetch=1, grid=(1,),
            in_specs=[
                pl.BlockSpec(pair.shape, lambda i, at: (0, 0, 0)), pl.BlockSpec((COMP, rows), lambda i, at: (0, at[0])),
            ],
            out_specs=(pl.BlockSpec((rows, LANES), lambda i, at: (0, 0)),) * 3,
        ),
        compiler_params=pltpu.CompilerParams(vmem_limit_bytes=60 << 20), name="points",
    )(spot, pair, components)
    other = lax.ppermute(mine, SAMP[1], [(0, 1), (1, 0)])
    place, meta, digits = pl.pallas_call(
        count_kernel,
        out_shape=(
            shape((groups, LANES), jnp.int32), shape((groups + 8, LANES), jnp.int32),
            shape((groups, TAIL, LANES), BF16),
        ),
        in_specs=[vmem] * len(pieces), out_specs=(vmem, vmem, vmem), compiler_params=params, name="count",
    )(*pieces)
    total = meta[groups, 0]
    meta = meta[:groups, 0]
    free, logden = lax.cond(
        total <= SMALL,
        functools.partial(iterated, SMALL_ROWS), functools.partial(iterated, slot_rows),
        meta, mine, other, place, digits, head, points, dead,
    )
    return free.reshape(-1), exchanged(logden, STATE).reshape(-1)


def solution(mesh):
    torus = Mesh(mesh.devices.reshape(4, 2, 8, 4), ("samp_0", "samp_1", "state_0", "state_1"))
    placed = (P(None, SAMP), P(None, STATE), P(SAMP), P(SAMP))
    return jax.shard_map(
        shards, mesh=torus, in_specs=placed, out_specs=(P(STATE), P(SAMP)), check_vma=False
    )
```

profile of v0, /device:TPU:2, one launch (start us, length us, event | category | flops | bytes accessed | tf_op | source)
XLA Modules:
  0.0 107.9 jit_solution(2767672339518854728)
XLA Ops:
  0.6 0.0 copy-start
  0.7 0.7 copy-done
  1.4 24.1 %all_to_all.50 = bf16[32,32,128]{2,1,0:T(8,128)(2,1)S(1)} all-to-all(bf16[32,32,128]{2,1,0:T(8,128)(2,1)S(1)} %broadcast_in_dim.23), channel_id=1, replica_groups=mesh['samp_0'=4,'samp_1'=2,'state_0'=8,'state_1'=4] {'state_0','state_1'}, dimensions={0} | all-to-all | bytes 524288 | tf_op jit(solution)/shard_map/all_to_all | solution.py:33
  25.5 0.0 collective-permute-start.4
  25.5 0.7 add_bitcast_fusion.own_ref
  26.2 0.0 copy-start.1
  26.2 0.6 collective-permute-start
  26.8 0.8 collective-permute-done
  27.6 0.5 collective-permute-start.3
  28.1 2.4 %collective-permute-start.2 = (s32[2,2,256]{2,1,0:T(2,128)S(1)}, s32[2,2,256]{2,1,0:T(2,128)S(1)}, u32[]{:S(2)}, u32[]{:S(2)}) collective-permute-start(s32[2,2,256]{2,1,0:T(2,128)S(1)} %pad_add_fusion.refs_0_), channel_id=1, source_target_pairs={{0,128},{64,192},{128,0},{192,64},{1,129},{65,193},{129,1},{193,65... | collective-permute-start | bytes 12296 | tf_op jit(solution)/shard_map/ppermute | solution.py:490
  30.6 1.8 %collective-permute-start.1 = (s32[2,2,256]{2,1,0:T(2,128)S(1)}, s32[2,2,256]{2,1,0:T(2,128)S(1)}, u32[]{:S(2)}, u32[]{:S(2)}) collective-permute-start(s32[2,2,256]{2,1,0:T(2,128)S(1)} %pad_add_fusion.refs_0_), channel_id=1, source_target_pairs={{0,64},{64,128},{128,192},{192,0},{1,65},{65,129},{129,193},{193,1... | collective-permute-start | bytes 12296 | tf_op jit(solution)/shard_map/ppermute | solution.py:490
  32.4 0.6 pad_add_fusion.1.spot_ref
  32.9 0.0 copy-done.1
  32.9 2.0 %points.1 = (bf16[1024,128]{1,0:T(8,128)(2,1)S(1)}, bf16[1024,128]{1,0:T(8,128)(2,1)S(1)}, f32[1024,128]{1,0:T(8,128)S(1)}) custom-call(s32[2]{0:T(128)} %pad_add_fusion.1.spot_ref, s32[1,2,256]{2,1,0:T(2,128)} %copy-done.1, bf16[64,32768]{1,0:T(8,128)(2,1)} %block_ref.1), custom_call_target="tpu_custom_call" | custom-call | tf_op jit(solution)/shard_map/points/pallas_call | solution.py:491
  34.9 0.0 collective-permute-done.3.refs_3_
  34.9 0.0 collective-permute-done.2.refs_2_
  34.9 0.0 collective-permute-done.1.refs_1_
  34.9 0.6 count.1
  35.5 0.5 slice.10
  36.7 0.0 collective-permute-done.4
  36.7 56.7 %conditional.1 = (f32[32,8,128]{2,1,0:T(8,128)S(1)}, f32[128]{0:T(128)}) conditional(s32[]{:T(128)} %bitcast.7, (s32[40,128]{1,0:T(8,128)S(1)}, bf16[32,32,128]{2,1,0:T(8,128)(2,1)S(1)}, bf16[32,32,128]{2,1,0:T(8,128)(2,1)S(1)}, s32[32,128]{1,0:T(8,128)S(1)}, bf16[32,16,128]{2,1,0:T(8,128)(2,1)S(1)}, /*index=5*/bf16[1024,128]{1,0:T(8,128)(2,1)S(1)}, ...), branch_computations={%region_0.0_spmd, %region_5.0_spmd} | conditional | flops 338944 | bytes 3100952 | solution.py:514
  36.9 0.1 copy.7
  37.0 4.1 %first.3 = (f32[8,8,128]{2,1,0:T(8,128)S(1)}, f32[8,128]{1,0:T(8,128)S(1)}, bf16[4,64,256]{2,1,0:T(8,128)(2,1)S(1)}, bf16[1024,128]{1,0:T(8,128)(2,1)S(1)}, f32[1024,128]{1,0:T(8,128)S(1)}) custom-call(s32[32]{0:T(128)S(1)} %slice_bitcast_fusion.1.meta_ref, bf16[32,32,128]{2,1,0:T(8,128)(2,1)S(1)} %get-tuple-element.57.mine_ref, ...), custom_call_target="tpu_custom_call" | custom-call | tf_op jit(solution)/shard_map/cond/branch_1_fun/first/pallas_call | solution.py:437
  41.2 8.2 %all_to_all.46 = f32[8,8,128]{2,1,0:T(8,128)S(1)} all-to-all(f32[8,8,128]{2,1,0:T(8,128)S(1)} %get-tuple-element.64), channel_id=1, replica_groups=mesh['samp_0'=4,'samp_1'=2,'state_0'=8,'state_1'=4] {'samp_0','samp_1'}, dimensions={0} | all-to-all | bytes 65536 | tf_op jit(solution)/shard_map/cond/branch_1_fun/all_to_all | solution.py:33
  49.4 14.3 %all_to_all.47.logs_in_ref = f32[32,8,128]{2,1,0:T(8,128)S(1)} all-to-all(f32[32,8,128]{2,1,0:T(8,128)S(1)} %broadcast_in_dim.12), channel_id=1, replica_groups=mesh['samp_0'=4,'samp_1'=2,'state_0'=8,'state_1'=4] {'state_0','state_1'}, dimensions={0} | all-to-all | bytes 262144 | tf_op jit(solution)/shard_map/cond/branch_1_fun/all_to_all | solution.py:33
  63.6 6.2 %second.3 = f32[32,8,128]{2,1,0:T(8,128)S(1)} custom-call(f32[32,8,128]{2,1,0:T(8,128)S(1)} %all_to_all.47.logs_in_ref, bf16[32,32,128]{2,1,0:T(8,128)(2,1)S(1)} %get-tuple-element.57.mine_ref, bf16[32,32,128]{2,1,0:T(8,128)(2,1)S(1)} %get-tuple-element.58.other_ref, f32[8,128]{1,0:T(8,128)S(1)} %get-tuple-element.65.log_count_ref, ...), custom_call_target="tpu_custom_call" | custom-call | tf_op jit(solution)/shard_map/cond/branch_1_fun/second/pallas_call | solution.py:452
  69.8 13.9 %all_to_all.48 = f32[32,8,128]{2,1,0:T(8,128)S(1)} all-to-all(f32[32,8,128]{2,1,0:T(8,128)S(1)} %second.3), channel_id=1, replica_groups=mesh['samp_0'=4,'samp_1'=2,'state_0'=8,'state_1'=4] {'state_0','state_1'}, dimensions={0} | all-to-all | bytes 262144 | tf_op jit(solution)/shard_map/cond/branch_1_fun/all_to_all | solution.py:33
  83.8 7.8 %all_to_all.49.logs_in_ref = f32[8,8,128]{2,1,0:T(8,128)S(1)} all-to-all(f32[8,8,128]{2,1,0:T(8,128)S(1)} %broadcast_in_dim.13), channel_id=1, replica_groups=mesh['samp_0'=4,'samp_1'=2,'state_0'=8,'state_1'=4] {'samp_0','samp_1'}, dimensions={0} | all-to-all | bytes 65536 | tf_op jit(solution)/shard_map/cond/branch_1_fun/all_to_all | solution.py:33
  91.7 1.8 %third.3 = (f32[1,128]{1,0:T(1,128)}, f32[32,8,128]{2,1,0:T(8,128)S(1)}) custom-call(f32[8,8,128]{2,1,0:T(8,128)S(1)} %all_to_all.49.logs_in_ref, f32[8,128]{1,0:T(8,128)S(1)} %get-tuple-element.65.log_count_ref, bf16[4,64,256]{2,1,0:T(8,128)(2,1)S(1)} %get-tuple-element.66.coefs_ref, bf16[1024,128]{1,0:T(8,128)(2,1)S(1)} %get-tuple-element.61.head_ref, ...), custom_call_target="tpu_custom_call" | custom-call | tf_op jit(solution)/shard_map/cond/branch_1_fun/third/pallas_call | solution.py:463
  93.5 13.7 %all_to_all.51 = f32[32,8,128]{2,1,0:T(8,128)S(1)} all-to-all(f32[32,8,128]{2,1,0:T(8,128)S(1)} %get-tuple-element.88), channel_id=1, replica_groups=mesh['samp_0'=4,'samp_1'=2,'state_0'=8,'state_1'=4] {'state_0','state_1'}, dimensions={0} | all-to-all | bytes 262144 | tf_op jit(solution)/shard_map/all_to_all | solution.py:33
  107.2 0.7 copy.13
  (12 shorter events, 0.2 us)
Async XLA Ops:
  0.6 0.7 copy-start
  25.5 11.2 %collective-permute-start.4 = (bf16[32,32,128]{2,1,0:T(8,128)(2,1)S(1)}, bf16[32,32,128]{2,1,0:T(8,128)(2,1)S(1)}, u32[]{:S(2)}, u32[]{:S(2)}) collective-permute-start(bf16[32,32,128]{2,1,0:T(8,128)(2,1)S(1)} %all_to_all.50), channel_id=1, source_target_pairs={{0,32},{32,0},{1,33},{33,1},{2,34},{34,2},{3,35},{35,3},{4,36},{36... | collective-permute-start | bytes 786440 | tf_op jit(solution)/shard_map/ppermute | solution.py:503
  26.2 6.7 %copy-start.1 = (s32[1,2,256]{2,1,0:T(2,128)}, s32[1,2,256]{2,1,0:T(2,128)S(1)}, u32[]{:S(2)}) copy-start(s32[1,2,256]{2,1,0:T(2,128)S(1)} %add_bitcast_fusion.own_ref) | copy-start | bytes 6148
  26.2 1.4 %collective-permute-start = (s32[1,2,256]{2,1,0:T(2,128)S(1)}, s32[1,2,256]{2,1,0:T(2,128)S(1)}, u32[]{:S(2)}, u32[]{:S(2)}) collective-permute-start(s32[1,2,256]{2,1,0:T(2,128)S(1)} %add_bitcast_fusion.own_ref), channel_id=1, source_target_pairs={{0,32},{32,0},{1,33},{33,1},{2,34},{34,2},{3,35},{35,3},{4,36},{36... | collective-permute-start | bytes 6152 | tf_op jit(solution)/shard_map/ppermute | solution.py:487
  27.6 7.3 %collective-permute-start.3 = (s32[2,2,256]{2,1,0:T(2,128)S(1)}, s32[2,2,256]{2,1,0:T(2,128)S(1)}, u32[]{:S(2)}, u32[]{:S(2)}) collective-permute-start(s32[2,2,256]{2,1,0:T(2,128)S(1)} %pad_add_fusion.refs_0_), channel_id=1, source_target_pairs={{0,192},{64,0},{128,64},{192,128},{1,193},{65,1},{129,65},{193,129... | collective-permute-start | bytes 12296 | tf_op jit(solution)/shard_map/ppermute | solution.py:490
  28.1 6.8 %collective-permute-start.2 = (s32[2,2,256]{2,1,0:T(2,128)S(1)}, s32[2,2,256]{2,1,0:T(2,128)S(1)}, u32[]{:S(2)}, u32[]{:S(2)}) collective-permute-start(s32[2,2,256]{2,1,0:T(2,128)S(1)} %pad_add_fusion.refs_0_), channel_id=1, source_target_pairs={{0,128},{64,192},{128,0},{192,64},{1,129},{65,193},{129,1},{193,65... | collective-permute-start | bytes 12296 | tf_op jit(solution)/shard_map/ppermute | solution.py:490
  30.6 4.4 %collective-permute-start.1 = (s32[2,2,256]{2,1,0:T(2,128)S(1)}, s32[2,2,256]{2,1,0:T(2,128)S(1)}, u32[]{:S(2)}, u32[]{:S(2)}) collective-permute-start(s32[2,2,256]{2,1,0:T(2,128)S(1)} %pad_add_fusion.refs_0_), channel_id=1, source_target_pairs={{0,64},{64,128},{128,192},{192,0},{1,65},{65,129},{129,193},{193,1... | collective-permute-start | bytes 12296 | tf_op jit(solution)/shard_map/ppermute | solution.py:490
where the time goes:
time: 109 us; the launch traced here: 108 us
  blocking collectives  82 us (75%)
  Pallas kernels  14.7 us (13%)
  starting transfers between devices  5.34 us (5%)
  local copies, waits for them, and re-layouts  2.05 us (2%)
  other arithmetic  1.41 us (1%)
  between operations  1.35 us (1%)
    all_to_all x6, blocking collectives, exchanged(): return lax.all_to_all(copies, axes, split_axis=0, concat_axis=0, tiled=True)  82 us
    pallas_call x1, Pallas kernels, iterated(): pl.pallas_call(second_kernel, out_shape=shape((groups, slot_rows if slot_...  6.15 us
    ppermute x3, starting transfers between devices, shards(): pieces = [blocks] + [lax.ppermute(blocks, SAMP[0], turn) for turn in turns]  4.76 us
    pallas_call x1, Pallas kernels, iterated(): pl.pallas_call(first_kernel, out_shape=(shape((samps, slot_rows, LANES),...  4.13 us
  transfers between devices with their start and end apart: 5, of which 1 were waited for; matrix products, arithmetic and copies ran while one was open for 2% of the time, Pallas kernels for 2%

commit v1 on v0

--- a/solution.py
+++ b/solution.py
@@ -478,6 +478,7 @@
     slot_rows = min(samps * block_window.shape[0] // LANES, groups)
     shape = jax.ShapeDtypeStruct
     vmem = pl.BlockSpec(memory_space=pltpu.VMEM)
+    smem = pl.BlockSpec(memory_space=pltpu.SMEM)
     params = pltpu.CompilerParams(vmem_limit_bytes=24 << 20)
     spot = jnp.stack([position, core]).astype(jnp.int32)
 
@@ -491,15 +492,9 @@
     head, points, dead = pl.pallas_call(
         points_kernel,
         out_shape=(shape((rows, LANES), BF16), shape((rows, LANES), BF16), shape((rows, LANES), F32)),
-        grid_spec=pltpu.PrefetchScalarGridSpec(
-            num_scalar_prefetch=1, grid=(1,),
-            in_specs=[
-                pl.BlockSpec(pair.shape, lambda i, at: (0, 0, 0)), pl.BlockSpec((COMP, rows), lambda i, at: (0, at[0])),
-            ],
-            out_specs=(pl.BlockSpec((rows, LANES), lambda i, at: (0, 0)),) * 3,
-        ),
-        compiler_params=pltpu.CompilerParams(vmem_limit_bytes=60 << 20), name="points",
-    )(spot, pair, components)
+        in_specs=[smem, vmem, vmem], out_specs=(vmem, vmem, vmem),
+        compiler_params=params, name="points",
+    )(spot, pair, lax.dynamic_slice_in_dim(components, position * rows, rows, 1))
     other = lax.ppermute(mine, SAMP[1], [(0, 1), (1, 0)])
     place, meta, digits = pl.pallas_call(
         count_kernel,

time: 109 us -> 108 us (level)
  blocking collectives: 82 us -> 58.7 us
  waiting for transfers between devices: 0.83 us -> 12.9 us
  starting transfers between devices: 5.34 us -> 16.3 us
  local copies, waits for them, and re-layouts: 2.05 us -> 3.65 us
  Pallas kernels: 14.7 us -> 13.3 us
    all_to_all x6 -> x5, blocking collectives: 82 us -> 58.7 us  [exchanged(): return lax.all_to_all(copies, axes, split_axis=0, concat_axis=0, tiled=True)]
    all_to_all x0 -> x1, waiting for transfers between devices: none -> 12.1 us  [exchanged(): return lax.all_to_all(copies, axes, split_axis=0, concat_axis=0, tiled=True)]
    all_to_all x0 -> x1, starting transfers between devices: none -> 11.5 us  [exchanged(): return lax.all_to_all(copies, axes, split_axis=0, concat_axis=0, tiled=True)]
  transfers between devices with their start and end apart: 5 -> 6, of which waited for: 1 -> 2; matrix products, arithmetic and copies ran while one was open for 2% -> 2% of each run, Pallas kernels for 2% -> 1%
where the time goes in v1:
time: 108 us; the launch traced here: 107 us
  blocking collectives  58.7 us (54%)
  starting transfers between devices  16.3 us (15%)
  Pallas kernels  13.3 us (12%)
  waiting for transfers between devices  12.9 us (12%)
  local copies, waits for them, and re-layouts  3.65 us (3%)
  between operations  1.37 us (1%)
    all_to_all x5, blocking collectives, exchanged(): return lax.all_to_all(copies, axes, split_axis=0, concat_axis=0, tiled=True)  58.7 us
    all_to_all x1, waiting for transfers between devices, exchanged(): return lax.all_to_all(copies, axes, split_axis=0, concat_axis=0, tiled=True)  12.1 us
    all_to_all x1, starting transfers between devices, exchanged(): return lax.all_to_all(copies, axes, split_axis=0, concat_axis=0, tiled=True)  11.5 us
    pallas_call x1, Pallas kernels, iterated(): pl.pallas_call(second_kernel, out_shape=shape((groups, slot_rows if slot_...  5.89 us
    ppermute x3, starting transfers between devices, shards(): pieces = [blocks] + [lax.ppermute(blocks, SAMP[0], turn) for turn in turns]  4.83 us
    pallas_call x1, Pallas kernels, iterated(): pl.pallas_call(first_kernel, out_shape=(shape((samps, slot_rows, LANES),...  4.12 us
  transfers between devices with their start and end apart: 6, of which 2 were waited for; matrix products, arithmetic and copies ran while one was open for 2% of the time, Pallas kernels for 1%

profile of v1, /device:TPU:2, one launch (start us, length us, event | category | flops | bytes accessed | tf_op | source)
XLA Modules:
  0.0 107.4 jit_solution(12893511669717679637)
XLA Ops:
  0.6 0.0 copy-start
  0.7 0.7 copy-done
  1.4 0.7 broadcast_in_dim.23
  2.1 11.5 %all-to-all-start.8 = ((bf16[32,32,128]{2,1,0:T(8,128)(2,1)}), bf16[32,32,128]{2,1,0:T(8,128)(2,1)S(1)}, u32[]{:S(2)}, u32[]{:S(2)}) async-start(bf16[32,32,128]{2,1,0:T(8,128)(2,1)} %broadcast_in_dim.23), calls=%async_computation.8 | async-start | bytes 524288 | tf_op jit(solution)/shard_map/all_to_all | solution.py:33
  13.6 0.7 add_bitcast_fusion.own_ref
  14.3 0.0 collective-permute-start
  14.3 12.1 %all-to-all-done.8 = bf16[32,32,128]{2,1,0:T(8,128)(2,1)S(1)} async-done(((bf16[32,32,128]{2,1,0:T(8,128)(2,1)}), bf16[32,32,128]{2,1,0:T(8,128)(2,1)S(1)}, u32[]{:S(2)}, u32[]{:S(2)}) %all-to-all-start.8) | async-done | bytes 262176 | tf_op jit(solution)/shard_map/all_to_all | solution.py:33
  26.4 0.0 collective-permute-start.4
  26.4 0.9 constant_dynamic-slice_fusion.block_ref
  27.3 0.0 collective-permute-done
  27.3 0.6 collective-permute-start.3
  27.9 2.4 %collective-permute-start.2 = (s32[2,2,256]{2,1,0:T(2,128)S(1)}, s32[2,2,256]{2,1,0:T(2,128)S(1)}, u32[]{:S(2)}, u32[]{:S(2)}) collective-permute-start(s32[2,2,256]{2,1,0:T(2,128)S(1)} %pad_add_fusion.refs_0_), channel_id=1, source_target_pairs={{0,128},{64,192},{128,0},{192,64},{1,129},{65,193},{129,1},{193,65... | collective-permute-start | bytes 12296 | tf_op jit(solution)/shard_map/ppermute | solution.py:491
  30.4 1.8 %collective-permute-start.1 = (s32[2,2,256]{2,1,0:T(2,128)S(1)}, s32[2,2,256]{2,1,0:T(2,128)S(1)}, u32[]{:S(2)}, u32[]{:S(2)}) collective-permute-start(s32[2,2,256]{2,1,0:T(2,128)S(1)} %pad_add_fusion.refs_0_), channel_id=1, source_target_pairs={{0,64},{64,128},{128,192},{192,0},{1,65},{65,129},{129,193},{193,1... | collective-permute-start | bytes 12296 | tf_op jit(solution)/shard_map/ppermute | solution.py:491
  32.2 0.1 pad_add_fusion.1.spot_ref
  32.2 0.9 points.1
  33.2 0.0 collective-permute-done.3.refs_3_
  33.2 0.0 collective-permute-done.2.refs_2_
  33.2 0.8 collective-permute-done.1.refs_1_
  34.0 0.6 count.1
  34.6 0.5 slice.10
  35.7 0.0 collective-permute-done.4
  35.7 57.2 %conditional.1 = (f32[32,8,128]{2,1,0:T(8,128)S(1)}, f32[128]{0:T(128)}) conditional(s32[]{:T(128)} %bitcast.7, (s32[40,128]{1,0:T(8,128)S(1)}, bf16[32,32,128]{2,1,0:T(8,128)(2,1)S(1)}, bf16[32,32,128]{2,1,0:T(8,128)(2,1)S(1)}, s32[32,128]{1,0:T(8,128)S(1)}, bf16[32,16,128]{2,1,0:T(8,128)(2,1)S(1)}, /*index=5*/bf16[1024,128]{1,0:T(8,128)(2,1)S(1)}, ...), branch_computations={%region_0.0_spmd, %region_5.0_spmd} | conditional | flops 338944 | bytes 3100952 | solution.py:509
  35.9 0.1 copy.7
  36.0 4.1 %first.3 = (f32[8,8,128]{2,1,0:T(8,128)S(1)}, f32[8,128]{1,0:T(8,128)S(1)}, bf16[4,64,256]{2,1,0:T(8,128)(2,1)S(1)}, bf16[1024,128]{1,0:T(8,128)(2,1)S(1)}, f32[1024,128]{1,0:T(8,128)S(1)}) custom-call(s32[32]{0:T(128)S(1)} %slice_bitcast_fusion.1.meta_ref, bf16[32,32,128]{2,1,0:T(8,128)(2,1)S(1)} %get-tuple-element.57.mine_ref, ...), custom_call_target="tpu_custom_call" | custom-call | tf_op jit(solution)/shard_map/cond/branch_1_fun/first/pallas_call | solution.py:437
  40.2 8.9 %all_to_all.46 = f32[8,8,128]{2,1,0:T(8,128)S(1)} all-to-all(f32[8,8,128]{2,1,0:T(8,128)S(1)} %get-tuple-element.64), channel_id=1, replica_groups=mesh['samp_0'=4,'samp_1'=2,'state_0'=8,'state_1'=4] {'samp_0','samp_1'}, dimensions={0} | all-to-all | bytes 65536 | tf_op jit(solution)/shard_map/cond/branch_1_fun/all_to_all | solution.py:33
  49.2 14.3 %all_to_all.47.logs_in_ref = f32[32,8,128]{2,1,0:T(8,128)S(1)} all-to-all(f32[32,8,128]{2,1,0:T(8,128)S(1)} %broadcast_in_dim.12), channel_id=1, replica_groups=mesh['samp_0'=4,'samp_1'=2,'state_0'=8,'state_1'=4] {'state_0','state_1'}, dimensions={0} | all-to-all | bytes 262144 | tf_op jit(solution)/shard_map/cond/branch_1_fun/all_to_all | solution.py:33
  63.4 5.9 %second.3 = f32[32,8,128]{2,1,0:T(8,128)S(1)} custom-call(f32[32,8,128]{2,1,0:T(8,128)S(1)} %all_to_all.47.logs_in_ref, bf16[32,32,128]{2,1,0:T(8,128)(2,1)S(1)} %get-tuple-element.57.mine_ref, bf16[32,32,128]{2,1,0:T(8,128)(2,1)S(1)} %get-tuple-element.58.other_ref, f32[8,128]{1,0:T(8,128)S(1)} %get-tuple-element.65.log_count_ref, ...), custom_call_target="tpu_custom_call" | custom-call | tf_op jit(solution)/shard_map/cond/branch_1_fun/second/pallas_call | solution.py:452
  69.3 13.9 %all_to_all.48 = f32[32,8,128]{2,1,0:T(8,128)S(1)} all-to-all(f32[32,8,128]{2,1,0:T(8,128)S(1)} %second.3), channel_id=1, replica_groups=mesh['samp_0'=4,'samp_1'=2,'state_0'=8,'state_1'=4] {'state_0','state_1'}, dimensions={0} | all-to-all | bytes 262144 | tf_op jit(solution)/shard_map/cond/branch_1_fun/all_to_all | solution.py:33
  83.3 7.8 %all_to_all.49.logs_in_ref = f32[8,8,128]{2,1,0:T(8,128)S(1)} all-to-all(f32[8,8,128]{2,1,0:T(8,128)S(1)} %broadcast_in_dim.13), channel_id=1, replica_groups=mesh['samp_0'=4,'samp_1'=2,'state_0'=8,'state_1'=4] {'samp_0','samp_1'}, dimensions={0} | all-to-all | bytes 65536 | tf_op jit(solution)/shard_map/cond/branch_1_fun/all_to_all | solution.py:33
  91.2 1.8 %third.3 = (f32[1,128]{1,0:T(1,128)}, f32[32,8,128]{2,1,0:T(8,128)S(1)}) custom-call(f32[8,8,128]{2,1,0:T(8,128)S(1)} %all_to_all.49.logs_in_ref, f32[8,128]{1,0:T(8,128)S(1)} %get-tuple-element.65.log_count_ref, bf16[4,64,256]{2,1,0:T(8,128)(2,1)S(1)} %get-tuple-element.66.coefs_ref, bf16[1024,128]{1,0:T(8,128)(2,1)S(1)} %get-tuple-element.61.head_ref, ...), custom_call_target="tpu_custom_call" | custom-call | tf_op jit(solution)/shard_map/cond/branch_1_fun/third/pallas_call | solution.py:463
  93.0 13.7 %all_to_all.50 = f32[32,8,128]{2,1,0:T(8,128)S(1)} all-to-all(f32[32,8,128]{2,1,0:T(8,128)S(1)} %get-tuple-element.88), channel_id=1, replica_groups=mesh['samp_0'=4,'samp_1'=2,'state_0'=8,'state_1'=4] {'state_0','state_1'}, dimensions={0} | all-to-all | bytes 262144 | tf_op jit(solution)/shard_map/all_to_all | solution.py:33
  106.7 0.7 copy.13
  (11 shorter events, 0.2 us)
Async XLA Ops:
  0.6 0.7 copy-start
  2.1 24.3 %all-to-all-start.8 = ((bf16[32,32,128]{2,1,0:T(8,128)(2,1)}), bf16[32,32,128]{2,1,0:T(8,128)(2,1)S(1)}, u32[]{:S(2)}, u32[]{:S(2)}) async-start(bf16[32,32,128]{2,1,0:T(8,128)(2,1)} %broadcast_in_dim.23), calls=%async_computation.8 | async-start | bytes 524288 | tf_op jit(solution)/shard_map/all_to_all | solution.py:33
  14.3 13.0 %collective-permute-start = (s32[1,2,256]{2,1,0:T(2,128)S(1)}, s32[1,2,256]{2,1,0:T(2,128)S(1)}, u32[]{:S(2)}, u32[]{:S(2)}) collective-permute-start(s32[1,2,256]{2,1,0:T(2,128)S(1)} %add_bitcast_fusion.own_ref), channel_id=1, source_target_pairs={{0,32},{32,0},{1,33},{33,1},{2,34},{34,2},{3,35},{35,3},{4,36},{36... | collective-permute-start | bytes 6152 | tf_op jit(solution)/shard_map/ppermute | solution.py:488
  26.4 9.3 %collective-permute-start.4 = (bf16[32,32,128]{2,1,0:T(8,128)(2,1)S(1)}, bf16[32,32,128]{2,1,0:T(8,128)(2,1)S(1)}, u32[]{:S(2)}, u32[]{:S(2)}) collective-permute-start(bf16[32,32,128]{2,1,0:T(8,128)(2,1)S(1)} %all-to-all-done.8), channel_id=1, source_target_pairs={{0,32},{32,0},{1,33},{33,1},{2,34},{34,2},{3,35},{35,3},{4,36},{36... | collective-permute-start | bytes 786440 | tf_op jit(solution)/shard_map/ppermute | solution.py:498
  27.3 5.8 %collective-permute-start.3 = (s32[2,2,256]{2,1,0:T(2,128)S(1)}, s32[2,2,256]{2,1,0:T(2,128)S(1)}, u32[]{:S(2)}, u32[]{:S(2)}) collective-permute-start(s32[2,2,256]{2,1,0:T(2,128)S(1)} %pad_add_fusion.refs_0_), channel_id=1, source_target_pairs={{0,192},{64,0},{128,64},{192,128},{1,193},{65,1},{129,65},{193,129... | collective-permute-start | bytes 12296 | tf_op jit(solution)/shard_map/ppermute | solution.py:491
  27.9 5.2 %collective-permute-start.2 = (s32[2,2,256]{2,1,0:T(2,128)S(1)}, s32[2,2,256]{2,1,0:T(2,128)S(1)}, u32[]{:S(2)}, u32[]{:S(2)}) collective-permute-start(s32[2,2,256]{2,1,0:T(2,128)S(1)} %pad_add_fusion.refs_0_), channel_id=1, source_target_pairs={{0,128},{64,192},{128,0},{192,64},{1,129},{65,193},{129,1},{193,65... | collective-permute-start | bytes 12296 | tf_op jit(solution)/shard_map/ppermute | solution.py:491
  30.4 3.6 %collective-permute-start.1 = (s32[2,2,256]{2,1,0:T(2,128)S(1)}, s32[2,2,256]{2,1,0:T(2,128)S(1)}, u32[]{:S(2)}, u32[]{:S(2)}) collective-permute-start(s32[2,2,256]{2,1,0:T(2,128)S(1)} %pad_add_fusion.refs_0_), channel_id=1, source_target_pairs={{0,64},{64,128},{128,192},{192,0},{1,65},{65,129},{129,193},{193,1... | collective-permute-start | bytes 12296 | tf_op jit(solution)/shard_map/ppermute | solution.py:491

commit v2 on v1

--- a/solution.py
+++ b/solution.py
@@ -54,11 +54,6 @@
     rest = x - high
     middle = rest.astype(BF16).astype(F32)
     return high, middle, rest - middle
-
-
-def log_sum(logs):
-    highest = jnp.max(logs, axis=0)
-    return highest + jnp.log(jnp.sum(jnp.exp(logs - highest[None]), axis=0))
 
 
 def log_sum_pieces(logs_ref):
@@ -334,6 +329,19 @@
         )
 
 
+def merge_kernel(logs_ref, copies_ref):
+    copies_ref[...] = jnp.broadcast_to(log_sum_pieces(logs_ref)[None], copies_ref.shape)
+
+
+def merged(logs, axes):
+    vmem = pl.BlockSpec(memory_space=pltpu.VMEM)
+    return pl.pallas_call(
+        merge_kernel, out_shape=jax.ShapeDtypeStruct((lax.axis_size(axes), *logs.shape[1:]), F32),
+        in_specs=[vmem], out_specs=vmem,
+        compiler_params=pltpu.CompilerParams(vmem_limit_bytes=24 << 20), name="merge",
+    )(logs)
+
+
 def places(slot_rows):
     if slot_rows == SMALL_ROWS:
         return (slot_rows - 1, slot_rows - 2), LANES - 1
@@ -447,8 +455,7 @@
         ],
         compiler_params=params, name="first",
     )(meta, mine, other, place, digits, head, points, dead)
-    logs = log_sum(exchanged(logs, SAMP))
-    logs = copies_of_each(logs, STATE)
+    logs = exchanged(merged(exchanged(logs, SAMP), STATE), STATE)
     logs = pl.pallas_call(
         second_kernel,
         out_shape=shape((groups, slot_rows if slot_rows == SMALL_ROWS else slot_rows + 8, LANES), F32),
@@ -459,7 +466,7 @@
         ],
         compiler_params=params, name="second",
     )(logs, mine, other, log_count, coefs, head, points, dead, anchored, base)
-    logs = copies_of_each(log_sum(exchanged(logs, STATE)), SAMP)
+    logs = exchanged(merged(exchanged(logs, STATE), SAMP), SAMP)
     return pl.pallas_call(
         third_kernel,
         out_shape=(shape((1, LANES), F32), shape((groups, rows // LANES, LANES), F32)),

time: 108 us -> 108 us (level)
  no operation moved by 1% of the time
where the time goes in v2:
time: 108 us; the launch traced here: 107 us
  blocking collectives  58.7 us (54%)
  starting transfers between devices  16.3 us (15%)
  Pallas kernels  13.4 us (12%)
  waiting for transfers between devices  12.9 us (12%)
  local copies, waits for them, and re-layouts  3.64 us (3%)
  between operations  1.37 us (1%)
    all_to_all x5, blocking collectives, exchanged(): return lax.all_to_all(copies, axes, split_axis=0, concat_axis=0, tiled=True)  58.7 us
    all_to_all x1, waiting for transfers between devices, exchanged(): return lax.all_to_all(copies, axes, split_axis=0, concat_axis=0, tiled=True)  12.1 us
    all_to_all x1, starting transfers between devices, exchanged(): return lax.all_to_all(copies, axes, split_axis=0, concat_axis=0, tiled=True)  11.5 us
    pallas_call x1, Pallas kernels, iterated(): pl.pallas_call(second_kernel, out_shape=shape((groups, slot_rows if slot_...  5.88 us
    ppermute x3, starting transfers between devices, shards(): pieces = [blocks] + [lax.ppermute(blocks, SAMP[0], turn) for turn in turns]  4.83 us
    pallas_call x1, Pallas kernels, iterated(): pl.pallas_call(first_kernel, out_shape=(shape((samps, slot_rows, LANES),...  4.11 us
  transfers between devices with their start and end apart: 6, of which 2 were waited for; matrix products, arithmetic and copies ran while one was open for 2% of the time, Pallas kernels for 1%

profile of v2, /device:TPU:2, one launch (start us, length us, event | category | flops | bytes accessed | tf_op | source)
XLA Modules:
  0.0 107.3 jit_solution(8566012947155676469)
XLA Ops:
  0.6 0.0 copy-start
  0.7 0.7 copy-done
  1.4 0.7 broadcast_in_dim.7
  2.1 11.5 %all-to-all-start.8 = ((bf16[32,32,128]{2,1,0:T(8,128)(2,1)}), bf16[32,32,128]{2,1,0:T(8,128)(2,1)S(1)}, u32[]{:S(2)}, u32[]{:S(2)}) async-start(bf16[32,32,128]{2,1,0:T(8,128)(2,1)} %broadcast_in_dim.7), calls=%async_computation.8 | async-start | bytes 524288 | tf_op jit(solution)/shard_map/all_to_all | solution.py:33
  13.6 0.7 add_bitcast_fusion.own_ref
  14.3 0.0 collective-permute-start
  14.3 12.1 %all-to-all-done.8 = bf16[32,32,128]{2,1,0:T(8,128)(2,1)S(1)} async-done(((bf16[32,32,128]{2,1,0:T(8,128)(2,1)}), bf16[32,32,128]{2,1,0:T(8,128)(2,1)S(1)}, u32[]{:S(2)}, u32[]{:S(2)}) %all-to-all-start.8) | async-done | bytes 262176 | tf_op jit(solution)/shard_map/all_to_all | solution.py:33
  26.4 0.0 collective-permute-start.4
  26.4 0.9 constant_dynamic-slice_fusion.block_ref
  27.3 0.0 collective-permute-done
  27.3 0.6 collective-permute-start.3
  27.9 2.4 %collective-permute-start.2 = (s32[2,2,256]{2,1,0:T(2,128)S(1)}, s32[2,2,256]{2,1,0:T(2,128)S(1)}, u32[]{:S(2)}, u32[]{:S(2)}) collective-permute-start(s32[2,2,256]{2,1,0:T(2,128)S(1)} %pad_add_fusion.refs_0_), channel_id=1, source_target_pairs={{0,128},{64,192},{128,0},{192,64},{1,129},{65,193},{129,1},{193,65... | collective-permute-start | bytes 12296 | tf_op jit(solution)/shard_map/ppermute | solution.py:498
  30.4 1.8 %collective-permute-start.1 = (s32[2,2,256]{2,1,0:T(2,128)S(1)}, s32[2,2,256]{2,1,0:T(2,128)S(1)}, u32[]{:S(2)}, u32[]{:S(2)}) collective-permute-start(s32[2,2,256]{2,1,0:T(2,128)S(1)} %pad_add_fusion.refs_0_), channel_id=1, source_target_pairs={{0,64},{64,128},{128,192},{192,0},{1,65},{65,129},{129,193},{193,1... | collective-permute-start | bytes 12296 | tf_op jit(solution)/shard_map/ppermute | solution.py:498
  32.2 0.1 pad_add_fusion.1.spot_ref
  32.2 0.9 points.1
  33.2 0.0 collective-permute-done.3.refs_3_
  33.2 0.8 collective-permute-done.1.refs_1_
  34.0 0.6 count.1
  34.6 0.5 slice.10
  35.7 0.0 collective-permute-done.4
  35.7 57.2 %conditional.1 = (f32[32,8,128]{2,1,0:T(8,128)S(1)}, f32[128]{0:T(128)}) conditional(s32[]{:T(128)} %bitcast.7, (s32[40,128]{1,0:T(8,128)S(1)}, bf16[32,32,128]{2,1,0:T(8,128)(2,1)S(1)}, bf16[32,32,128]{2,1,0:T(8,128)(2,1)S(1)}, s32[32,128]{1,0:T(8,128)S(1)}, bf16[32,16,128]{2,1,0:T(8,128)(2,1)S(1)}, /*index=5*/bf16[1024,128]{1,0:T(8,128)(2,1)S(1)}, ...), branch_computations={%region_0.0_spmd, %region_1.0_spmd} | conditional | bytes 1679632 | solution.py:516
  35.9 0.1 copy.7
  36.1 4.1 %first.3 = (f32[8,8,128]{2,1,0:T(8,128)S(1)}, f32[8,128]{1,0:T(8,128)S(1)}, bf16[4,64,256]{2,1,0:T(8,128)(2,1)S(1)}, bf16[1024,128]{1,0:T(8,128)(2,1)S(1)}, f32[1024,128]{1,0:T(8,128)S(1)}) custom-call(s32[32]{0:T(128)S(1)} %slice_bitcast_fusion.1.meta_ref, bf16[32,32,128]{2,1,0:T(8,128)(2,1)S(1)} %get-tuple-element.57.mine_ref, ...), custom_call_target="tpu_custom_call" | custom-call | tf_op jit(solution)/shard_map/cond/branch_1_fun/first/pallas_call | solution.py:445
  40.2 8.9 %all_to_all.46.logs_ref = f32[8,8,128]{2,1,0:T(8,128)S(1)} all-to-all(f32[8,8,128]{2,1,0:T(8,128)S(1)} %get-tuple-element.64), channel_id=1, replica_groups=mesh['samp_0'=4,'samp_1'=2,'state_0'=8,'state_1'=4] {'samp_0','samp_1'}, dimensions={0} | all-to-all | bytes 65536 | tf_op jit(solution)/shard_map/cond/branch_1_fun/all_to_all | solution.py:33
  49.1 14.3 %all_to_all.47.logs_in_ref = f32[32,8,128]{2,1,0:T(8,128)S(1)} all-to-all(f32[32,8,128]{2,1,0:T(8,128)S(1)} %merge.6), channel_id=1, replica_groups=mesh['samp_0'=4,'samp_1'=2,'state_0'=8,'state_1'=4] {'state_0','state_1'}, dimensions={0} | all-to-all | bytes 262144 | tf_op jit(solution)/shard_map/cond/branch_1_fun/all_to_all | solution.py:33
  63.4 5.9 %second.3 = f32[32,8,128]{2,1,0:T(8,128)S(1)} custom-call(f32[32,8,128]{2,1,0:T(8,128)S(1)} %all_to_all.47.logs_in_ref, bf16[32,32,128]{2,1,0:T(8,128)(2,1)S(1)} %get-tuple-element.57.mine_ref, bf16[32,32,128]{2,1,0:T(8,128)(2,1)S(1)} %get-tuple-element.58.other_ref, f32[8,128]{1,0:T(8,128)S(1)} %get-tuple-element.65.log_count_ref, ...), custom_call_target="tpu_custom_call" | custom-call | tf_op jit(solution)/shard_map/cond/branch_1_fun/second/pallas_call | solution.py:459
  69.3 13.9 %all_to_all.48.logs_ref = f32[32,8,128]{2,1,0:T(8,128)S(1)} all-to-all(f32[32,8,128]{2,1,0:T(8,128)S(1)} %second.3), channel_id=1, replica_groups=mesh['samp_0'=4,'samp_1'=2,'state_0'=8,'state_1'=4] {'state_0','state_1'}, dimensions={0} | all-to-all | bytes 262144 | tf_op jit(solution)/shard_map/cond/branch_1_fun/all_to_all | solution.py:33
  83.2 0.1 merge.7
  83.3 7.8 %all_to_all.49.logs_in_ref = f32[8,8,128]{2,1,0:T(8,128)S(1)} all-to-all(f32[8,8,128]{2,1,0:T(8,128)S(1)} %merge.7), channel_id=1, replica_groups=mesh['samp_0'=4,'samp_1'=2,'state_0'=8,'state_1'=4] {'samp_0','samp_1'}, dimensions={0} | all-to-all | bytes 65536 | tf_op jit(solution)/shard_map/cond/branch_1_fun/all_to_all | solution.py:33
  91.1 1.8 %third.3 = (f32[1,128]{1,0:T(1,128)}, f32[32,8,128]{2,1,0:T(8,128)S(1)}) custom-call(f32[8,8,128]{2,1,0:T(8,128)S(1)} %all_to_all.49.logs_in_ref, f32[8,128]{1,0:T(8,128)S(1)} %get-tuple-element.65.log_count_ref, bf16[4,64,256]{2,1,0:T(8,128)(2,1)S(1)} %get-tuple-element.66.coefs_ref, bf16[1024,128]{1,0:T(8,128)(2,1)S(1)} %get-tuple-element.61.head_ref, ...), custom_call_target="tpu_custom_call" | custom-call | tf_op jit(solution)/shard_map/cond/branch_1_fun/third/pallas_call | solution.py:470
  92.9 13.7 %all_to_all.50 = f32[32,8,128]{2,1,0:T(8,128)S(1)} all-to-all(f32[32,8,128]{2,1,0:T(8,128)S(1)} %get-tuple-element.88), channel_id=1, replica_groups=mesh['samp_0'=4,'samp_1'=2,'state_0'=8,'state_1'=4] {'state_0','state_1'}, dimensions={0} | all-to-all | bytes 262144 | tf_op jit(solution)/shard_map/all_to_all | solution.py:33
  106.7 0.7 copy.13
  (5 shorter events, 0.0 us)
Async XLA Ops:
  0.6 0.7 copy-start
  2.1 24.3 %all-to-all-start.8 = ((bf16[32,32,128]{2,1,0:T(8,128)(2,1)}), bf16[32,32,128]{2,1,0:T(8,128)(2,1)S(1)}, u32[]{:S(2)}, u32[]{:S(2)}) async-start(bf16[32,32,128]{2,1,0:T(8,128)(2,1)} %broadcast_in_dim.7), calls=%async_computation.8 | async-start | bytes 524288 | tf_op jit(solution)/shard_map/all_to_all | solution.py:33
  14.3 13.0 %collective-permute-start = (s32[1,2,256]{2,1,0:T(2,128)S(1)}, s32[1,2,256]{2,1,0:T(2,128)S(1)}, u32[]{:S(2)}, u32[]{:S(2)}) collective-permute-start(s32[1,2,256]{2,1,0:T(2,128)S(1)} %add_bitcast_fusion.own_ref), channel_id=1, source_target_pairs={{0,32},{32,0},{1,33},{33,1},{2,34},{34,2},{3,35},{35,3},{4,36},{36... | collective-permute-start | bytes 6152 | tf_op jit(solution)/shard_map/ppermute | solution.py:495
  26.4 9.3 %collective-permute-start.4 = (bf16[32,32,128]{2,1,0:T(8,128)(2,1)S(1)}, bf16[32,32,128]{2,1,0:T(8,128)(2,1)S(1)}, u32[]{:S(2)}, u32[]{:S(2)}) collective-permute-start(bf16[32,32,128]{2,1,0:T(8,128)(2,1)S(1)} %all-to-all-done.8), channel_id=1, source_target_pairs={{0,32},{32,0},{1,33},{33,1},{2,34},{34,2},{3,35},{35,3},{4,36},{36... | collective-permute-start | bytes 786440 | tf_op jit(solution)/shard_map/ppermute | solution.py:505
  27.3 5.8 %collective-permute-start.3 = (s32[2,2,256]{2,1,0:T(2,128)S(1)}, s32[2,2,256]{2,1,0:T(2,128)S(1)}, u32[]{:S(2)}, u32[]{:S(2)}) collective-permute-start(s32[2,2,256]{2,1,0:T(2,128)S(1)} %pad_add_fusion.refs_0_), channel_id=1, source_target_pairs={{0,192},{64,0},{128,64},{192,128},{1,193},{65,1},{129,65},{193,129... | collective-permute-start | bytes 12296 | tf_op jit(solution)/shard_map/ppermute | solution.py:498
  27.9 5.2 %collective-permute-start.2 = (s32[2,2,256]{2,1,0:T(2,128)S(1)}, s32[2,2,256]{2,1,0:T(2,128)S(1)}, u32[]{:S(2)}, u32[]{:S(2)}) collective-permute-start(s32[2,2,256]{2,1,0:T(2,128)S(1)} %pad_add_fusion.refs_0_), channel_id=1, source_target_pairs={{0,128},{64,192},{128,0},{192,64},{1,129},{65,193},{129,1},{193,65... | collective-permute-start | bytes 12296 | tf_op jit(solution)/shard_map/ppermute | solution.py:498
  30.4 3.6 %collective-permute-start.1 = (s32[2,2,256]{2,1,0:T(2,128)S(1)}, s32[2,2,256]{2,1,0:T(2,128)S(1)}, u32[]{:S(2)}, u32[]{:S(2)}) collective-permute-start(s32[2,2,256]{2,1,0:T(2,128)S(1)} %pad_add_fusion.refs_0_), channel_id=1, source_target_pairs={{0,64},{64,128},{128,192},{192,0},{1,65},{65,129},{129,193},{193,1... | collective-permute-start | bytes 12296 | tf_op jit(solution)/shard_map/ppermute | solution.py:498
